TPU v7x, 32 devices: a whole 2x2x4 slice. The times are simulated.
32 devices in a mesh: row: 4 (over x, core), col: 8 (over z, y).
Axes of the slice: x: 2, y: 2, z: 4, core: 2. Of those that a mesh axis runs over, the one named last changes fastest.
Arguments:
- train_docs: bfloat16 [32768, 768], P(('row', 'col')), may hold values from -85 to 85
- eval_rows: bfloat16 [2048, 768], P(('row', 'col')), may hold values from -85 to 85
- bench_ids: int32 [2048, 1], P(('row', 'col')), may hold values from 0 to 127
Outputs:
- row_best: float32 [32768], P(('row', 'col'))
- bench_best: float32 [128], replicated
Inputs may be any that keep to these rules, and one draw needn't show every extreme that they name: `bench_ids`: every benchmark has at least one question.
All inputs are finite; a program needn't handle non-finite values.
Results may differ from a plain program's by a relative error of at most 0.0003.
Values may be sent and summed in bfloat16 or wider, within the bound.
A program may use at most 64 MiB of HBM per device.

v0:
```python
import math

import jax
import jax.numpy as jnp
from jax import lax
from jax.sharding import PartitionSpec as P

NBENCH = 128


epsilon = 1e-06


def scales(embedded):
    squares = jnp.mean(jnp.square(embedded.astype(jnp.float32)), axis=1)
    return lax.rsqrt(squares + epsilon) / math.sqrt(embedded.shape[1])


def bench_max(column_best, labels, count):
    matches = labels[:, None] == jnp.arange(count, dtype=jnp.int32)[None, :]
    return jnp.max(jnp.where(matches, column_best[:, None], -jnp.inf), axis=0)


def make_absorb(documents, doc_scale, carried, pieces, offset):
    best_row, best_col, label_vec = carried
    portion, portion_ids = pieces
    products = lax.dot_general(
        documents, portion, (((1,), (1,)), ((), ())), preferred_element_type=jnp.float32
    )
    scored = products * doc_scale[:, None] * scales(portion)[None, :]
    best_row = jnp.max(scored, axis=1)
    best_col = jnp.max(scored, axis=0)
    label_vec = lax.dynamic_update_slice_in_dim(label_vec, portion_ids[:, 0], offset, 0)
    return (best_row, best_col, label_vec)


def starting_carry(doc_count, question_count):
    return (
        jnp.full((doc_count,), -jnp.inf, jnp.float32),
        jnp.full((question_count,), -jnp.inf, jnp.float32),
        jnp.zeros((question_count,), jnp.int32),
    )


def body(train_docs, eval_rows, bench_ids):
    own_rows = eval_rows.shape[0]
    own_docs = train_docs.shape[0]
    groups_col = lax.axis_size("col")
    documents = lax.all_gather(train_docs, "row", axis=0, tiled=True)
    doc_scale = scales(documents)
    band = own_rows * groups_col
    wide_row, column_vec, label_vec = make_absorb(
        documents,
        doc_scale,
        starting_carry(documents.shape[0], band),
        (
            lax.all_gather(eval_rows, "col", axis=0, tiled=True),
            lax.all_gather(bench_ids, "col", axis=0, tiled=True),
        ),
        jnp.int32(0),
    )
    row_index = lax.axis_index("row")
    wide_all = lax.pmax(wide_row, "row")
    best_row = lax.dynamic_slice_in_dim(wide_all, row_index * own_docs, own_docs, 0)
    column_band = lax.pmax(column_vec, "col")
    bench_best = lax.pmax(bench_max(column_band, label_vec, NBENCH), "row")
    return (best_row, bench_best)


def solution(mesh):
    in_specs = (P(("row", "col"), None), P(("row", "col"), None), P(("row", "col"), None))
    out_specs = (P(("row", "col")), P())
    return jax.shard_map(body, mesh=mesh, in_specs=in_specs, out_specs=out_specs, check_vma=False)
```

profile of v0, /device:TPU:0, one launch (start us, length us, event | category | flops | bytes accessed | tf_op | source)
XLA Modules:
  0.0 107.3 jit_solution(1623280842982379394)
XLA Ops:
  7.2 0.0 all-gather.2.cloned.1.call-start
  7.2 0.7 all-gather.2.cloned.1.call-update
  7.9 1.2 %dynamic-slice = u32[1]{0:T(128)} dynamic-slice(u32[32]{0:T(128)} %constant.30, u32[]{:T(128)S(6)} %add.28), dynamic_slice_sizes={1} | dynamic-slice | bytes 12
  9.8 0.8 bitcast_dynamic-update-slice_fusion
  10.6 13.1 %all-reduce = s32[512]{0:T(512)S(1)} all-reduce(s32[512]{0:T(512)S(1)} %bitcast_dynamic-update-slice_fusion), channel_id=1, replica_groups=mesh['row'=4,'col'=8] {'col'}, use_global_device_ids=true, to_apply=%add | all-reduce | flops 512 | bytes 4096
  23.6 32.4 %all_gather.10 = bf16[512,768]{1,0:T(8,128)(2,1)S(1)} all-gather(bf16[64,768]{1,0:T(8,128)(2,1)} %param.4), channel_id=1, replica_groups=mesh['row'=4,'col'=8] {'col'}, dimensions={0}, use_global_device_ids=true | all-gather | bytes 884736 | tf_op jit(solution)/shard_map/all_gather | solution.py:57
  56.0 0.2 multiply_reduce_fusion.1
  56.3 2.4 %all-gather.2.cloned.1.call-done = bf16[4096,768]{1,0:T(8,128)(2,1)} async-done(((bf16[1024,768]{1,0:T(8,128)(2,1)}), bf16[4096,768]{1,0:T(8,128)(2,1)}) %all-gather.2.cloned.1.call-update) | async-done | bytes 6291472 | tf_op jit(solution)/shard_map/all_gather | solution.py:49
  58.6 0.0 copy-start
  58.6 4.2 %multiply_reduce_fusion = f32[4096]{0:T(1024)S(1)} fusion(bf16[4096,768]{1,0:T(8,128)(2,1)} %all-gather.2.cloned.1.call-done), kind=kLoop, calls=%fused_computation | loop fusion | flops 9433088 | bytes 6307840 | tf_op jit(solution)/shard_map/reduce_sum | solution.py:15
  62.9 0.3 copy-done
  63.2 4.2 %fusion = (f32[512]{0:T(512)S(1)}, f32[4096]{0:T(1024)S(1)}) fusion(f32[512]{0:T(512)S(1)} %rsqrt_multiply_fusion.1, f32[4096]{0:T(1024)S(1)} %rsqrt_multiply_fusion, bf16[4096,768]{1,0:T(8,128)(2,1)S(1)} %copy-done, bf16[512,768]{1,0:T(8,128)(2,1)S(1)} %all_gather.10), kind=kOutput, calls=%fused_computation.2 | convolution fusion | flops 3229609472 | bytes 7114752 | tf_op jit(solution)/shard_map/dot_general | solution.py:27
  67.5 21.4 %pmax.22 = f32[512]{0:T(512)S(1)} all-reduce(f32[512]{0:T(512)S(1)} %get-tuple-element.2), channel_id=1, replica_groups=mesh['row'=4,'col'=8] {'col'}, use_global_device_ids=true, to_apply=%region_5.0 | all-reduce | flops 512 | bytes 4096 | tf_op jit(solution)/shard_map/pmax | solution.py:65
  88.8 0.2 select_reduce_fusion
  89.0 10.8 %all-reduce.1 = (f32[4096]{0:T(1024)S(1)}, f32[128]{0:T(128)}) all-reduce(f32[4096]{0:T(1024)S(1)} %get-tuple-element.3, f32[128]{0:T(128)S(1)} %select_reduce_fusion), channel_id=1, replica_groups=mesh['row'=4,'col'=8] {'row'}, use_global_device_ids=true, to_apply=%region_3.0 | all-reduce | flops 4224 | bytes 33792 | tf_op jit(solution)/shard_map/pmax | solution.py:63
  99.9 0.6 dynamic_slice.3
  (3 shorter events, 0.0 us)
Async XLA Ops:
  7.2 51.5 %all-gather.2.cloned.1.call-start = ((), (), s32[]{:S(2)}) async-start(), calls=%async_computation | async-start | bytes 7864320 | tf_op jit(solution)/shard_map/all_gather | solution.py:49
  58.6 4.6 %copy-start = (bf16[4096,768]{1,0:T(8,128)(2,1)S(1)}, bf16[4096,768]{1,0:T(8,128)(2,1)}, u32[]{:S(2)}) copy-start(bf16[4096,768]{1,0:T(8,128)(2,1)} %all-gather.2.cloned.1.call-done) | copy-start | bytes 18874372
Sparse Core Ops, SparseCore 0:
  9.5 49.0 all-gather.1
where the time goes:
time: 108 us; the launch traced here: 107 us
  blocking collectives  77.7 us (72%)
  between operations  14.7 us (14%)
  other arithmetic  4.7 us (4%)
  matrix products  4.2 us (4%)
  waiting for transfers between devices  3.08 us (3%)
  local copies, waits for them, and re-layouts  2.93 us (3%)
    all_gather x1, blocking collectives, body(): lax.all_gather(eval_rows, 'col', axis=0, tiled=True)  32.4 us
    pmax x1, blocking collectives, body(): column_band = lax.pmax(column_vec, 'col')  21.4 us
    unnamed x1, blocking collectives  13.1 us
    pmax x1, blocking collectives, body(): wide_all = lax.pmax(wide_row, 'row')  10.8 us
    reduce_sum x2, other arithmetic, scales(): squares = jnp.mean(jnp.square(embedded.astype(jnp.float32)), axis=1)  4.46 us
    dot_general x1, matrix products, make_absorb(): lax.dot_general(documents, portion, (((1,), (1,)), ((), ())), preferred_e...  4.2 us
    all_gather x1, waiting for transfers between devices, body(): documents = lax.all_gather(train_docs, 'row', axis=0, tiled=True)  2.4 us
    unnamed x5, local copies, waits for them, and re-layouts  2.34 us
  transfers between devices with their start and end apart: 1, of which 1 were waited for; matrix products, arithmetic and copies ran while one was open for 2% of the time, Pallas kernels for 0%

commit v1 on v0

v1 whole, which is shorter than its diff:
```python
import math

import jax
import jax.numpy as jnp
from jax import lax
from jax.sharding import PartitionSpec as P

NBENCH = 128


epsilon = 1e-06


def scales(embedded):
    squares = jnp.mean(jnp.square(embedded.astype(jnp.float32)), axis=1)
    return lax.rsqrt(squares + epsilon) / math.sqrt(embedded.shape[1])


def bench_max(column_best, labels, count):
    matches = labels[:, None] == jnp.arange(count, dtype=jnp.int32)[None, :]
    return jnp.max(jnp.where(matches, column_best[:, None], -jnp.inf), axis=0)


def body(train_docs, eval_rows, bench_ids):
    questions = lax.all_gather(eval_rows, ("row", "col"), axis=0, tiled=True)
    labels = lax.all_gather(bench_ids[:, 0], ("row", "col"), axis=0, tiled=True)
    products = lax.dot_general(
        train_docs, questions, (((1,), (1,)), ((), ())), preferred_element_type=jnp.float32
    )
    scored = products * scales(train_docs)[:, None] * scales(questions)[None, :]
    best_row = jnp.max(scored, axis=1)
    best_col = jnp.max(scored, axis=0)
    bench_best = lax.pmax(bench_max(best_col, labels, NBENCH), ("row", "col"))
    return (best_row, bench_best)


def solution(mesh):
    in_specs = (P(("row", "col"), None), P(("row", "col"), None), P(("row", "col"), None))
    out_specs = (P(("row", "col")), P())
    return jax.shard_map(body, mesh=mesh, in_specs=in_specs, out_specs=out_specs, check_vma=False)
```

time: 108 us -> 126 us (1.17)
  waiting for transfers between devices: 3.08 us -> 21 us
  blocking collectives: 77.7 us -> 80.2 us
  local copies, waits for them, and re-layouts: 2.93 us -> 0.87 us
    all_gather x1 -> x0, blocking collectives: 32.4 us -> none  [body(): lax.all_gather(eval_rows, 'col', axis=0, tiled=True)]
    unnamed x1, blocking collectives: 13.1 us -> 42.1 us
    all_gather x1, waiting for transfers between devices: 2.4 us -> 20.3 us  [body(): questions = lax.all_gather(eval_rows, ('row', 'col'), axis=0, tiled=True)]
    pmax x2 -> x1, blocking collectives: 32.2 us -> 38 us  [body(): bench_best = lax.pmax(bench_max(best_col, labels, NBENCH), ('row', 'col'))]
    unnamed x5 -> x6, local copies, waits for them, and re-layouts: 2.34 us -> 0.87 us
where the time goes in v1:
time: 126 us
  blocking collectives  80.2 us (64%)
  waiting for transfers between devices  21 us (17%)
  between operations  14.1 us (11%)
  other arithmetic  5.22 us (4%)
  matrix products  4.48 us (4%)
    unnamed x1, blocking collectives  42.1 us
    pmax x1, blocking collectives, body(): bench_best = lax.pmax(bench_max(best_col, labels, NBENCH), ('row', 'col'))  38 us
    all_gather x1, waiting for transfers between devices, body(): questions = lax.all_gather(eval_rows, ('row', 'col'), axis=0, tiled=True)  20.3 us
    reduce_sum x2, other arithmetic, scales(): squares = jnp.mean(jnp.square(embedded.astype(jnp.float32)), axis=1)  4.5 us
    dot_general x1, matrix products, body(): lax.dot_general(train_docs, questions, (((1,), (1,)), ((), ())), preferre...  4.48 us
  transfers between devices with their start and end apart: 1, of which 1 were waited for; matrix products, arithmetic and copies ran while one was open for 2% of the time, Pallas kernels for 0%

profile of v1, /device:TPU:0, one launch (start us, length us, event | category | flops | bytes accessed | tf_op | source)
XLA Modules:
  0.0 125.8 jit_solution(9610568163043381752)
XLA Ops:
  7.2 0.0 copy-start.1
  7.2 0.0 all-gather.3.cloned.1.call-start
  7.2 0.7 all-gather.3.cloned.1.call-update
  7.9 0.8 bitcast_dynamic-update-slice_fusion
  8.7 42.1 %all-reduce = s32[2048]{0:T(1024)S(1)} all-reduce(s32[2048]{0:T(1024)S(1)} %bitcast_dynamic-update-slice_fusion), channel_id=2, replica_groups=mesh['row'=4,'col'=8] {'row','col'}, use_global_device_ids=true, to_apply=%add | all-reduce | flops 2048 | bytes 16384
  50.8 1.8 %multiply_reduce_fusion.1 = f32[1024]{0:T(1024)S(1)} fusion(bf16[1024,768]{1,0:T(8,128)(2,1)} %param.3), kind=kLoop, calls=%fused_computation.4 | loop fusion | flops 2358272 | bytes 1576960 | tf_op jit(solution)/shard_map/reduce_sum | solution.py:15
  52.6 20.3 %all-gather.3.cloned.1.call-done = bf16[2048,768]{1,0:T(8,128)(2,1)} async-done(((bf16[64,768]{1,0:T(8,128)(2,1)}), bf16[2048,768]{1,0:T(8,128)(2,1)}) %all-gather.3.cloned.1.call-update) | async-done | bytes 3145744 | tf_op jit(solution)/shard_map/all_gather | solution.py:25
  72.9 0.0 copy-start
  72.9 2.7 %multiply_reduce_fusion = f32[2048]{0:T(1024)S(1)} fusion(bf16[2048,768]{1,0:T(8,128)(2,1)} %all-gather.3.cloned.1.call-done), kind=kLoop, calls=%fused_computation.3 | loop fusion | flops 4716544 | bytes 3153920 | tf_op jit(solution)/shard_map/reduce_sum | solution.py:15
  75.7 0.0 copy-done.1
  75.7 0.1 copy-done
  75.8 4.5 %fusion = (f32[2048]{0:T(1024)S(1)}, f32[1024]{0:T(1024)}) fusion(f32[2048]{0:T(1024)S(1)} %rsqrt_multiply_fusion, f32[1024]{0:T(1024)S(1)} %rsqrt_multiply_fusion.1, bf16[1024,768]{1,0:T(8,128)(2,1)S(1)} %copy-done.1, bf16[2048,768]{1,0:T(8,128)(2,1)S(1)} %copy-done), kind=kOutput, calls=%fused_computation.1 | convolution fusion | flops 3229611008 | bytes 4743168 | tf_op jit(solution)/shard_map/dot_general | solution.py:27
  80.2 0.7 select_reduce_fusion
  80.9 38.0 %pmax.7 = f32[128]{0:T(128)} all-reduce(f32[128]{0:T(128)S(1)} %select_reduce_fusion), channel_id=1, replica_groups=mesh['row'=4,'col'=8] {'row','col'}, use_global_device_ids=true, to_apply=%region_5.6 | all-reduce | flops 128 | bytes 1024 | tf_op jit(solution)/shard_map/pmax | solution.py:33
  (3 shorter events, 0.0 us)
Async XLA Ops:
  7.2 68.5 %copy-start.1 = (bf16[1024,768]{1,0:T(8,128)(2,1)S(1)}, bf16[1024,768]{1,0:T(8,128)(2,1)}, u32[]{:S(2)}) copy-start(bf16[1024,768]{1,0:T(8,128)(2,1)} %param.3) | copy-start | bytes 4718596
  7.2 65.7 %all-gather.3.cloned.1.call-start = ((), (), s32[]{:S(2)}) async-start(), calls=%async_computation | async-start | bytes 3244032 | tf_op jit(solution)/shard_map/all_gather | solution.py:25
  72.9 2.8 %copy-start = (bf16[2048,768]{1,0:T(8,128)(2,1)S(1)}, bf16[2048,768]{1,0:T(8,128)(2,1)}, u32[]{:S(2)}) copy-start(bf16[2048,768]{1,0:T(8,128)(2,1)} %all-gather.3.cloned.1.call-done) | copy-start | bytes 9437188
Sparse Core Ops, SparseCore 0:
  10.9 61.9 all-gather.2

commit v2 on v1

v2 whole, which is shorter than its diff:
```python
import functools
import math

import jax
import jax.numpy as jnp
from jax import lax
from jax.experimental import pallas as pl
from jax.experimental.pallas import tpu as pltpu
from jax.sharding import PartitionSpec as P

NBENCH = 128
CORES = 2
PARTS = 4
TILE = 256
LANES = 128

epsilon = 1e-06
MESH = pl.DeviceIdType.MESH


def fold_lanes(values, op):
    total = values[:, :LANES]
    for start in range(LANES, values.shape[1], LANES):
        total = op(total, values[:, start : start + LANES])
    return total


def square_sums(rows):
    wide = rows.astype(jnp.float32)
    return fold_lanes(wide * wide, jnp.add)


def to_scale(sums, width):
    return lax.rsqrt(sums / width + epsilon) / math.sqrt(width)


def kernel(dims, docs_hbm, eval_ref, ids_ref, row_out, bench_out, docs, held, labels, doc_scale,
           row_max, row_part, row_other, bench_acc, stage_col, stage_row, local_sem, send_sem, recv_sem):
    X, Z, Y = dims
    R, C = X * CORES, Z * Y
    row, col = lax.axis_index("row"), lax.axis_index("col")
    x, core = row // CORES, lax.rem(row, CORES)
    z, y = col // Y, lax.rem(col, Y)
    partner = x * CORES + (1 - core)
    n_docs, width = docs_hbm.shape
    piece = eval_ref.shape[0] // PARTS
    sizes = {"x": X, "y": Y, "z": Z}
    place = {"x": x, "y": y, "z": z}
    counter = [0]
    started = []

    def device(dim, step):
        moved = dict(place)
        moved[dim] = lax.rem(place[dim] + step + sizes[dim], sizes[dim])
        return {"row": moved["x"] * CORES + core, "col": moved["z"] * Y + moved["y"]}

    def send(src, dst, target):
        i = counter[0]
        counter[0] += 1
        copy = pltpu.make_async_remote_copy(
            src_ref=src, dst_ref=dst, send_sem=send_sem.at[i], recv_sem=recv_sem.at[i],
            device_id=target, device_id_type=MESH,
        )
        copy.start()
        started.append(copy)
        return copy

    barrier = pltpu.get_barrier_semaphore()
    for k in range(1, R):
        pl.semaphore_signal(barrier, inc=1, device_id={"row": lax.rem(row + k, R), "col": col}, device_id_type=MESH)
    for k in range(1, C):
        pl.semaphore_signal(barrier, inc=1, device_id={"row": row, "col": lax.rem(col + k, C)}, device_id_type=MESH)

    own_docs = pltpu.make_async_copy(docs_hbm, docs.at[core], local_sem.at[PARTS + 1])
    own_docs.start()
    locals_ = [
        pltpu.make_async_copy(eval_ref.at[pl.ds(q * piece, piece)], held.at[q, x, z, y], local_sem.at[q])
        for q in range(PARTS)
    ]
    locals_.append(pltpu.make_async_copy(ids_ref, labels.at[x, col], local_sem.at[PARTS]))
    for copy in locals_:
        copy.start()
    for copy in locals_:
        copy.wait()
    pl.semaphore_wait(barrier, R + C - 2)

    def gather(q, order):
        where = dict(place)
        for dim in order:
            n = sizes[dim]
            last = n // 2
            for step in range(1, last + 1):
                copies = []
                split = n % 2 == 0 and step == last and n > 2
                for sign in (1, -1):
                    if n == 2 and sign < 0:
                        continue
                    where[dim] = lax.rem(place[dim] - sign * (step - 1) + n, n)
                    ref = held.at[q, where["x"], where["z"], where["y"]]
                    if split:
                        half = width // 2
                        ref = held.at[q, where["x"], where["z"], where["y"], ..., pl.ds(0 if sign > 0 else half, half)]
                    copies.append(send(ref, ref, device(dim, sign)))
                yield
                for copy in copies:
                    copy.wait_recv()
            where[dim] = slice(None)

    runs = [gather(q, order) for q, order in enumerate(("xyz", "yxz", "zxy", "zyx"))]
    for run in runs:
        next(run, None)
    doc_copy = send(docs_hbm, docs.at[core], {"row": partner, "col": col})
    id_copies = [
        send(labels.at[x, col], labels.at[x, col], {"row": row, "col": lax.rem(col + k, C)}) for k in range(1, C)
    ]

    live = list(runs)
    first = True
    while live:
        keep = []
        for run in live:
            try:
                next(run)
                keep.append(run)
            except StopIteration:
                pass
        live = keep
        if first:
            first = False
            for copy in id_copies:
                copy.wait_recv()
            id_copies = [
                send(labels.at[x], labels.at[x], {"row": lax.rem(x + k, X) * CORES + core, "col": col})
                for k in range(1, X)
            ]
            own_docs.wait()
            doc_copy.wait_recv()
            for c in range(CORES):

                @pl.loop(0, n_docs // TILE)
                def _(t):
                    rows = pl.ds(pl.multiple_of(t * TILE, TILE), TILE)
                    sums = jnp.sum(square_sums(docs[c, rows, :]), axis=1, keepdims=True)
                    doc_scale[c, rows, :] = jnp.broadcast_to(to_scale(sums, width), (TILE, LANES))
                    row_max[c, rows, :] = jnp.full((TILE, LANES), -jnp.inf, jnp.float32)

            bench_acc[...] = jnp.full(bench_acc.shape, -jnp.inf, jnp.float32)
    for copy in id_copies:
        copy.wait_recv()

    owners = X * C
    chunk = owners * piece
    ids = labels[...].reshape(owners, ids_ref.shape[1]).astype(jnp.float32).astype(jnp.bfloat16)
    slot = lax.broadcasted_iota(jnp.int32, (ids_ref.shape[1], chunk), 0)
    lane = lax.broadcasted_iota(jnp.int32, (ids_ref.shape[1], chunk), 1)
    owner = lax.broadcasted_iota(jnp.int32, (owners, chunk), 0)
    owner_lane = lax.broadcasted_iota(jnp.int32, (owners, chunk), 1)
    bench = lax.broadcasted_iota(jnp.int32, (NBENCH, chunk), 0).astype(jnp.float32)
    for q in range(PARTS):
        questions = held[q].reshape(chunk, width)
        sums = jnp.sum(square_sums(questions).T, axis=0, keepdims=True)
        eval_scale = to_scale(sums, width)
        best = jnp.full((8, chunk), -jnp.inf, jnp.float32)
        for c in range(CORES):

            def absorb(t, best, c=c, questions=questions, eval_scale=eval_scale):
                rows = pl.ds(pl.multiple_of(t * TILE, TILE), TILE)
                products = lax.dot_general(
                    docs[c, rows, :], questions, (((1,), (1,)), ((), ())), preferred_element_type=jnp.float32
                )
                scored = products * eval_scale
                row_max[c, rows, :] = jnp.maximum(row_max[c, rows, :], fold_lanes(scored, jnp.maximum))
                scale = jnp.concatenate([doc_scale[c, rows, :]] * (chunk // LANES), axis=1)
                scored = scored * scale
                return jnp.maximum(best, jnp.max(scored.reshape(TILE // 8, 8, chunk), axis=0))

            best = lax.fori_loop(0, n_docs // TILE, absorb, best)
        column = jnp.max(best, axis=0, keepdims=True)
        spread = jnp.where(slot == q * piece + lax.rem(lane, piece), 1.0, 0.0).astype(jnp.bfloat16)
        placed = jnp.dot(ids, spread, preferred_element_type=jnp.float32)
        label = jnp.max(jnp.where(owner == owner_lane // piece, placed, -1.0), axis=0, keepdims=True)
        matched = jnp.where(bench == label, column, -jnp.inf)
        bench_acc[...] = jnp.maximum(bench_acc[...], fold_lanes(matched, jnp.maximum))

    mine = jnp.max(bench_acc[...].T, axis=0, keepdims=True)
    stage_col[col] = mine
    col_copies = [
        send(stage_col.at[col], stage_col.at[col], {"row": row, "col": lax.rem(col + k, C)}) for k in range(1, C)
    ]
    for c in range(CORES):
        for t in range(n_docs // LANES):
            rows = slice(t * LANES, (t + 1) * LANES)
            block = row_max[c, rows, :] * doc_scale[c, rows, :]
            row_part[c, t : t + 1, :] = jnp.max(block.T, axis=0, keepdims=True)
    row_copy = send(row_part.at[1 - core], row_other, {"row": partner, "col": col})
    for copy in col_copies:
        copy.wait_recv()
    mine = jnp.max(stage_col[...], axis=0)
    stage_row[row] = mine
    row_copies = [
        send(stage_row.at[row], stage_row.at[row], {"row": lax.rem(row + k, R), "col": col}) for k in range(1, R)
    ]
    row_copy.wait_recv()
    row_out[...] = jnp.maximum(row_part[core], row_other[...])
    for copy in row_copies:
        copy.wait_recv()
    bench_out[...] = jnp.max(stage_row[...], axis=0)
    for copy in started:
        copy.wait_send()


def split_col(size):
    best = 1
    for candidate in range(1, size + 1):
        if size % candidate == 0 and candidate * candidate <= size:
            best = candidate
    return best


def body(dims, train_docs, eval_rows, bench_ids):
    X, Z, Y = dims
    n_docs, width = train_docs.shape
    own = eval_rows.shape[0]
    R, C = X * CORES, Z * Y
    owners = X * C
    copies = 4 * PARTS * (X + Y + Z) + 2 * (R + C) + 4
    f32 = jnp.float32
    row_best, bench_best = pl.pallas_call(
        functools.partial(kernel, dims),
        out_shape=(
            jax.ShapeDtypeStruct((n_docs // LANES, LANES), f32),
            jax.ShapeDtypeStruct((1, NBENCH), f32),
        ),
        in_specs=[
            pl.BlockSpec(memory_space=pl.ANY),
            pl.BlockSpec(memory_space=pltpu.VMEM),
            pl.BlockSpec(memory_space=pltpu.VMEM),
        ],
        out_specs=(pl.BlockSpec(memory_space=pltpu.VMEM), pl.BlockSpec(memory_space=pltpu.VMEM)),
        scratch_shapes=[
            pltpu.VMEM((CORES, n_docs, width), train_docs.dtype),
            pltpu.VMEM((PARTS, X, Z, Y, own // PARTS, width), eval_rows.dtype),
            pltpu.VMEM((X, C, 1, own), jnp.int32),
            pltpu.VMEM((CORES, n_docs, LANES), f32),
            pltpu.VMEM((CORES, n_docs, LANES), f32),
            pltpu.VMEM((CORES, n_docs // LANES, LANES), f32),
            pltpu.VMEM((n_docs // LANES, LANES), f32),
            pltpu.VMEM((NBENCH, LANES), f32),
            pltpu.VMEM((C, 1, NBENCH), f32),
            pltpu.VMEM((R, 1, NBENCH), f32),
            pltpu.SemaphoreType.DMA((PARTS + 2,)),
            pltpu.SemaphoreType.DMA((copies,)),
            pltpu.SemaphoreType.DMA((copies,)),
        ],
        compiler_params=pltpu.CompilerParams(
            collective_id=0, has_side_effects=True, vmem_limit_bytes=48 * 1024 * 1024
        ),
    )(train_docs, eval_rows, bench_ids.reshape(1, own))
    return row_best.reshape(n_docs), bench_best.reshape(NBENCH)


def solution(mesh):
    columns = mesh.shape["col"]
    Y = split_col(columns)
    dims = (mesh.shape["row"] // CORES, columns // Y, Y)
    in_specs = (P(("row", "col"), None), P(("row", "col"), None), P(("row", "col"), None))
    out_specs = (P(("row", "col")), P())
    return jax.shard_map(
        functools.partial(body, dims), mesh=mesh, in_specs=in_specs, out_specs=out_specs, check_vma=False
    )
```

time: 126 us -> 54.7 us (0.43)
  blocking collectives: 80.2 us -> 0 us
  Pallas kernels: 0 us -> 49.8 us
  waiting for transfers between devices: 21 us -> 0 us
  between operations: 14.1 us -> 0.65 us
  other arithmetic: 5.22 us -> 0 us
  matrix products: 4.48 us -> 0 us
  local copies, waits for them, and re-layouts: 0.87 us -> 4.05 us
    pallas_call x0 -> x1, Pallas kernels: none -> 49.8 us  [body(): pl.pallas_call(functools.partial(kernel, dims), out_shape=(jax.ShapeDtype...]
    unnamed x1 -> x0, blocking collectives: 42.1 us -> none
    pmax x1 -> x0, blocking collectives: 38 us -> none  [body(): bench_best = lax.pmax(bench_max(best_col, labels, NBENCH), ('row', 'col'))]
    all_gather x1 -> x0, waiting for transfers between devices: 20.3 us -> none  [body(): questions = lax.all_gather(eval_rows, ('row', 'col'), axis=0, tiled=True)]
    reduce_sum x2 -> x0, other arithmetic: 4.5 us -> none  [scales(): squares = jnp.mean(jnp.square(embedded.astype(jnp.float32)), axis=1)]
    dot_general x1 -> x0, matrix products: 4.48 us -> none  [body(): lax.dot_general(train_docs, questions, (((1,), (1,)), ((), ())), preferre...]
    unnamed x6 -> x8, local copies, waits for them, and re-layouts: 0.87 us -> 4.05 us
  transfers between devices with their start and end apart: 1 -> 0, of which waited for: 1 -> 0; matrix products, arithmetic and copies ran while one was open for 2% -> 0% of each run, Pallas kernels for 0% -> 0%
where the time goes in v2:
time: 54.7 us; the launch traced here: 54.5 us
  Pallas kernels  49.8 us (91%)
  local copies, waits for them, and re-layouts  4.05 us (7%)
  between operations  0.65 us (1%)
    pallas_call x1, Pallas kernels, body(): pl.pallas_call(functools.partial(kernel, dims), out_shape=(jax.ShapeDtype...  49.8 us
    unnamed x8, local copies, waits for them, and re-layouts  4.05 us

profile of v2, /device:TPU:0, one launch (start us, length us, event | category | flops | bytes accessed | tf_op | source)
XLA Modules:
  0.0 54.5 jit_solution(14090363899025376110)
XLA Ops:
  0.6 0.0 copy-start
  0.6 1.4 %copy-done = bf16[1024,768]{1,0:T(8,128)(2,1)S(1)} copy-done((bf16[1024,768]{1,0:T(8,128)(2,1)S(1)}, bf16[1024,768]{1,0:T(8,128)(2,1)}, u32[]{:S(2)}) %copy-start) | copy-done | bytes 1572888
  2.0 0.0 copy-start.1
  2.0 0.9 %copy-done.1 = bf16[64,768]{1,0:T(8,128)(2,1)S(1)} copy-done((bf16[64,768]{1,0:T(8,128)(2,1)S(1)}, bf16[64,768]{1,0:T(8,128)(2,1)}, u32[]{:S(2)}) %copy-start.1) | copy-done | bytes 98328
  2.9 0.0 copy-start.2
  2.9 0.7 %copy-done.2 = s32[64,1]{0,1:T(1,128)S(1)} copy-done((s32[64,1]{0,1:T(1,128)S(1)}, s32[64,1]{0,1:T(1,128)}, u32[]{:S(2)}) %copy-start.2) | copy-done | bytes 280
  3.6 49.8 %shard_map.50 = (f32[8,128]{1,0:T(8,128)S(1)}, f32[1,128]{1,0:T(1,128)S(1)}) custom-call(bf16[1024,768]{1,0:T(8,128)(2,1)S(1)} %copy-done, bf16[64,768]{1,0:T(8,128)(2,1)S(1)} %copy-done.1, s32[1,64]{1,0:T(1,128)S(1)} %bitcast.4), custom_call_target="tpu_custom_call" | custom-call | tf_op jit(solution)/shard_map/pallas_call | solution.py:228
  53.4 0.6 %copy.7 = f32[1024]{0:T(1024)} copy(f32[1024]{0:T(1024)S(1)} %bitcast.3) | data formatting | bytes 8192
  54.0 0.5 copy.8
Async XLA Ops:
  0.6 1.4 %copy-start = (bf16[1024,768]{1,0:T(8,128)(2,1)S(1)}, bf16[1024,768]{1,0:T(8,128)(2,1)}, u32[]{:S(2)}) copy-start(bf16[1024,768]{1,0:T(8,128)(2,1)} %docs_hbm.1) | copy-start | bytes 4718596
  2.0 0.9 %copy-start.1 = (bf16[64,768]{1,0:T(8,128)(2,1)S(1)}, bf16[64,768]{1,0:T(8,128)(2,1)}, u32[]{:S(2)}) copy-start(bf16[64,768]{1,0:T(8,128)(2,1)} %eval_ref.1) | copy-start | bytes 294916
  2.9 0.7 %copy-start.2 = (s32[64,1]{0,1:T(1,128)S(1)}, s32[64,1]{0,1:T(1,128)}, u32[]{:S(2)}) copy-start(s32[64,1]{0,1:T(1,128)} %param.5) | copy-start | bytes 772

commit v3 on v2

--- a/solution.py
+++ b/solution.py
@@ -12,6 +12,7 @@
 CORES = 2
 PARTS = 4
 TILE = 256
+ROWS = 1024
 LANES = 128
 
 epsilon = 1e-06
@@ -106,7 +107,8 @@
                     copy.wait_recv()
             where[dim] = slice(None)
 
-    runs = [gather(q, order) for q, order in enumerate(("xyz", "yxz", "zxy", "zyx"))]
+    orders = ("zxy", "zyx", "xyz", "yxz")
+    runs = [gather(q, order) for q, order in enumerate(orders)]
     for run in runs:
         next(run, None)
     doc_copy = send(docs_hbm, docs.at[core], {"row": partner, "col": col})
@@ -115,7 +117,7 @@
     ]
 
     live = list(runs)
-    first = True
+    first, turn = True, 0
     while live:
         keep = []
         for run in live:
@@ -125,14 +127,16 @@
             except StopIteration:
                 pass
         live = keep
-        if first:
-            first = False
+        turn += 1
+        if turn == 2:
             for copy in id_copies:
                 copy.wait_recv()
             id_copies = [
                 send(labels.at[x], labels.at[x], {"row": lax.rem(x + k, X) * CORES + core, "col": col})
                 for k in range(1, X)
             ]
+        if first:
+            first = False
             own_docs.wait()
             doc_copy.wait_recv()
             for c in range(CORES):
@@ -148,6 +152,7 @@
     for copy in id_copies:
         copy.wait_recv()
 
+    tall = math.gcd(n_docs, ROWS)
     owners = X * C
     chunk = owners * piece
     ids = labels[...].reshape(owners, ids_ref.shape[1]).astype(jnp.float32).astype(jnp.bfloat16)
@@ -164,7 +169,7 @@
         for c in range(CORES):
 
             def absorb(t, best, c=c, questions=questions, eval_scale=eval_scale):
-                rows = pl.ds(pl.multiple_of(t * TILE, TILE), TILE)
+                rows = pl.ds(pl.multiple_of(t * tall, tall), tall)
                 products = lax.dot_general(
                     docs[c, rows, :], questions, (((1,), (1,)), ((), ())), preferred_element_type=jnp.float32
                 )
@@ -172,9 +177,9 @@
                 row_max[c, rows, :] = jnp.maximum(row_max[c, rows, :], fold_lanes(scored, jnp.maximum))
                 scale = jnp.concatenate([doc_scale[c, rows, :]] * (chunk // LANES), axis=1)
                 scored = scored * scale
-                return jnp.maximum(best, jnp.max(scored.reshape(TILE // 8, 8, chunk), axis=0))
-
-            best = lax.fori_loop(0, n_docs // TILE, absorb, best)
+                return jnp.maximum(best, jnp.max(scored.reshape(tall // 8, 8, chunk), axis=0))
+
+            best = lax.fori_loop(0, n_docs // tall, absorb, best)
         column = jnp.max(best, axis=0, keepdims=True)
         spread = jnp.where(slot == q * piece + lax.rem(lane, piece), 1.0, 0.0).astype(jnp.bfloat16)
         placed = jnp.dot(ids, spread, preferred_element_type=jnp.float32)
@@ -232,9 +237,9 @@
             jax.ShapeDtypeStruct((1, NBENCH), f32),
         ),
         in_specs=[
-            pl.BlockSpec(memory_space=pl.ANY),
-            pl.BlockSpec(memory_space=pltpu.VMEM),
-            pl.BlockSpec(memory_space=pltpu.VMEM),
+            pl.BlockSpec(memory_space=pltpu.HBM),
+            pl.BlockSpec(memory_space=pltpu.HBM),
+            pl.BlockSpec(memory_space=pltpu.HBM),
         ],
         out_specs=(pl.BlockSpec(memory_space=pltpu.VMEM), pl.BlockSpec(memory_space=pltpu.VMEM)),
         scratch_shapes=[

time: 54.7 us -> 46.8 us (0.86)
  Pallas kernels: 49.8 us -> 42 us
    pallas_call x1, Pallas kernels: 49.8 us -> 42 us  [body(): pl.pallas_call(functools.partial(kernel, dims), out_shape=(jax.ShapeDtype...]
where the time goes in v3:
time: 46.8 us; the launch traced here: 46.7 us
  Pallas kernels  42 us (90%)
  local copies, waits for them, and re-layouts  4.05 us (9%)
  between operations  0.65 us (1%)
    pallas_call x1, Pallas kernels, body(): pl.pallas_call(functools.partial(kernel, dims), out_shape=(jax.ShapeDtype...  42 us
    unnamed x8, local copies, waits for them, and re-layouts  4.05 us

profile of v3, /device:TPU:0, one launch (start us, length us, event | category | flops | bytes accessed | tf_op | source)
XLA Modules:
  0.0 46.7 jit_solution(15736499515879947526)
XLA Ops:
  0.6 0.0 copy-start
  0.6 1.4 %copy-done = bf16[1024,768]{1,0:T(8,128)(2,1)S(1)} copy-done((bf16[1024,768]{1,0:T(8,128)(2,1)S(1)}, bf16[1024,768]{1,0:T(8,128)(2,1)}, u32[]{:S(2)}) %copy-start) | copy-done | bytes 1572888
  2.0 0.0 copy-start.1
  2.0 0.9 %copy-done.1 = bf16[64,768]{1,0:T(8,128)(2,1)S(1)} copy-done((bf16[64,768]{1,0:T(8,128)(2,1)S(1)}, bf16[64,768]{1,0:T(8,128)(2,1)}, u32[]{:S(2)}) %copy-start.1) | copy-done | bytes 98328
  2.9 0.0 copy-start.2
  2.9 0.7 %copy-done.2 = s32[64,1]{0,1:T(1,128)S(1)} copy-done((s32[64,1]{0,1:T(1,128)S(1)}, s32[64,1]{0,1:T(1,128)}, u32[]{:S(2)}) %copy-start.2) | copy-done | bytes 280
  3.6 42.0 %shard_map.50 = (f32[8,128]{1,0:T(8,128)S(1)}, f32[1,128]{1,0:T(1,128)S(1)}) custom-call(bf16[1024,768]{1,0:T(8,128)(2,1)S(1)} %copy-done, bf16[64,768]{1,0:T(8,128)(2,1)S(1)} %copy-done.1, s32[1,64]{1,0:T(1,128)S(1)} %bitcast.4), custom_call_target="tpu_custom_call" | custom-call | tf_op jit(solution)/shard_map/pallas_call | solution.py:233
  45.6 0.6 %copy.7 = f32[1024]{0:T(1024)} copy(f32[1024]{0:T(1024)S(1)} %bitcast.3) | data formatting | bytes 8192
  46.1 0.5 %copy.8 = f32[128]{0:T(128)} copy(f32[128]{0:T(128)S(1)} %bitcast.5) | data formatting | bytes 1024
Async XLA Ops:
  0.6 1.4 %copy-start = (bf16[1024,768]{1,0:T(8,128)(2,1)S(1)}, bf16[1024,768]{1,0:T(8,128)(2,1)}, u32[]{:S(2)}) copy-start(bf16[1024,768]{1,0:T(8,128)(2,1)} %docs_hbm.1) | copy-start | bytes 4718596
  2.0 0.9 %copy-start.1 = (bf16[64,768]{1,0:T(8,128)(2,1)S(1)}, bf16[64,768]{1,0:T(8,128)(2,1)}, u32[]{:S(2)}) copy-start(bf16[64,768]{1,0:T(8,128)(2,1)} %eval_ref.1) | copy-start | bytes 294916
  2.9 0.7 %copy-start.2 = (s32[64,1]{0,1:T(1,128)S(1)}, s32[64,1]{0,1:T(1,128)}, u32[]{:S(2)}) copy-start(s32[64,1]{0,1:T(1,128)} %param.5) | copy-start | bytes 772

commit v4 on v3

--- a/solution.py
+++ b/solution.py
@@ -13,6 +13,7 @@
 PARTS = 4
 TILE = 256
 ROWS = 1024
+ORDERS = ("zxy", "zyx", "xyz", "yxz")
 LANES = 128
 
 epsilon = 1e-06
@@ -85,70 +86,67 @@
         copy.wait()
     pl.semaphore_wait(barrier, R + C - 2)
 
-    def gather(q, order):
-        where = dict(place)
-        for dim in order:
-            n = sizes[dim]
-            last = n // 2
-            for step in range(1, last + 1):
-                copies = []
-                split = n % 2 == 0 and step == last and n > 2
-                for sign in (1, -1):
-                    if n == 2 and sign < 0:
-                        continue
-                    where[dim] = lax.rem(place[dim] - sign * (step - 1) + n, n)
-                    ref = held.at[q, where["x"], where["z"], where["y"]]
-                    if split:
-                        half = width // 2
-                        ref = held.at[q, where["x"], where["z"], where["y"], ..., pl.ds(0 if sign > 0 else half, half)]
-                    copies.append(send(ref, ref, device(dim, sign)))
-                yield
-                for copy in copies:
-                    copy.wait_recv()
-            where[dim] = slice(None)
-
-    orders = ("zxy", "zyx", "xyz", "yxz")
-    runs = [gather(q, order) for q, order in enumerate(orders)]
-    for run in runs:
-        next(run, None)
-    doc_copy = send(docs_hbm, docs.at[core], {"row": partner, "col": col})
+    waiting = []
+
+    def emit(q, fixed, dim, later, step):
+        n = sizes[dim]
+        last = n // 2
+        if step > last:
+            return
+        split = n % 2 == 0 and step == last and n > 2
+        copies, arrivals = [], []
+        for sign in (1, -1) if n > 2 else (1,):
+            where = {**place, **fixed, dim: lax.rem(place[dim] - sign * (step - 1) + n, n)}
+            at = (q, where["x"], where["z"], where["y"])
+            if split:
+                half = width // 2
+                at += (slice(None), pl.ds(0 if sign > 0 else half, half))
+            copies.append(send(held.at[at], held.at[at], device(dim, sign)))
+            arrivals.append(lax.rem(place[dim] - sign * step + n, n))
+        waiting.append((q, fixed, dim, later, step, copies, arrivals[:1] if split else arrivals))
+
+    def advance():
+        q, fixed, dim, later, step, copies, arrivals = waiting.pop(0)
+        for copy in copies:
+            copy.wait_recv()
+        emit(q, fixed, dim, later, step + 1)
+        for position in arrivals:
+            for k, follow in enumerate(later):
+                emit(q, {**fixed, dim: position}, follow, later[k + 1 :], 1)
+
+    for level in range(3):
+        for q, order in enumerate(ORDERS):
+            emit(q, {}, order[level], order[level + 1 :], 1)
+        if level == 0:
+            doc_copy = send(docs_hbm, docs.at[core], {"row": partner, "col": col})
+            id_copies = [
+                send(labels.at[x, col], labels.at[x, col], {"row": row, "col": lax.rem(col + k, C)})
+                for k in range(1, C)
+            ]
+
+    for _ in range(len(waiting)):
+        advance()
+    for copy in id_copies:
+        copy.wait_recv()
     id_copies = [
-        send(labels.at[x, col], labels.at[x, col], {"row": row, "col": lax.rem(col + k, C)}) for k in range(1, C)
-    ]
-
-    live = list(runs)
-    first, turn = True, 0
-    while live:
-        keep = []
-        for run in live:
-            try:
-                next(run)
-                keep.append(run)
-            except StopIteration:
-                pass
-        live = keep
-        turn += 1
-        if turn == 2:
-            for copy in id_copies:
-                copy.wait_recv()
-            id_copies = [
-                send(labels.at[x], labels.at[x], {"row": lax.rem(x + k, X) * CORES + core, "col": col})
-                for k in range(1, X)
-            ]
-        if first:
-            first = False
-            own_docs.wait()
-            doc_copy.wait_recv()
-            for c in range(CORES):
-
-                @pl.loop(0, n_docs // TILE)
-                def _(t):
-                    rows = pl.ds(pl.multiple_of(t * TILE, TILE), TILE)
-                    sums = jnp.sum(square_sums(docs[c, rows, :]), axis=1, keepdims=True)
-                    doc_scale[c, rows, :] = jnp.broadcast_to(to_scale(sums, width), (TILE, LANES))
-                    row_max[c, rows, :] = jnp.full((TILE, LANES), -jnp.inf, jnp.float32)
-
-            bench_acc[...] = jnp.full(bench_acc.shape, -jnp.inf, jnp.float32)
+        send(labels.at[x], labels.at[x], {"row": lax.rem(x + k, X) * CORES + core, "col": col}) for k in range(1, X)
+    ]
+    own_docs.wait()
+    doc_copy.wait_recv()
+    bench_acc[...] = jnp.full(bench_acc.shape, -jnp.inf, jnp.float32)
+    for c in range(CORES):
+
+        @pl.loop(0, n_docs // TILE)
+        def _(t):
+            rows = pl.ds(pl.multiple_of(t * TILE, TILE), TILE)
+            sums = jnp.sum(square_sums(docs[c, rows, :]), axis=1, keepdims=True)
+            doc_scale[c, rows, :] = jnp.broadcast_to(to_scale(sums, width), (TILE, LANES))
+            row_max[c, rows, :] = jnp.full((TILE, LANES), -jnp.inf, jnp.float32)
+
+        for _ in range(len(waiting) // 2):
+            advance()
+    while waiting:
+        advance()
     for copy in id_copies:
         copy.wait_recv()
 
@@ -228,7 +226,10 @@
     own = eval_rows.shape[0]
     R, C = X * CORES, Z * Y
     owners = X * C
-    copies = 4 * PARTS * (X + Y + Z) + 2 * (R + C) + 4
+    sizes = {"x": X, "y": Y, "z": Z}
+    copies = 2 * (R + C) + 4
+    for a, b, c in ORDERS:
+        copies += sizes[a] * (1 + sizes[b] * (1 + sizes[c]))
     f32 = jnp.float32
     row_best, bench_best = pl.pallas_call(
         functools.partial(kernel, dims),

time: 46.8 us -> 42.9 us (0.917)
  Pallas kernels: 42 us -> 38 us
    pallas_call x1, Pallas kernels: 42 us -> 38 us  [body(): pl.pallas_call(functools.partial(kernel, dims), out_shape=(jax.ShapeDtype...]
where the time goes in v4:
time: 42.9 us; the launch traced here: 42.7 us
  Pallas kernels  38 us (89%)
  local copies, waits for them, and re-layouts  4.05 us (9%)
  between operations  0.65 us (2%)
    pallas_call x1, Pallas kernels, body(): pl.pallas_call(functools.partial(kernel, dims), out_shape=(jax.ShapeDtype...  38 us
    unnamed x8, local copies, waits for them, and re-layouts  4.05 us

profile of v4, /device:TPU:0, one launch (start us, length us, event | category | flops | bytes accessed | tf_op | source)
XLA Modules:
  0.0 42.7 jit_solution(6579008282319391504)
XLA Ops:
  0.6 0.0 copy-start
  0.6 1.4 %copy-done = bf16[1024,768]{1,0:T(8,128)(2,1)S(1)} copy-done((bf16[1024,768]{1,0:T(8,128)(2,1)S(1)}, bf16[1024,768]{1,0:T(8,128)(2,1)}, u32[]{:S(2)}) %copy-start) | copy-done | bytes 1572888
  2.0 0.0 copy-start.1
  2.0 0.9 %copy-done.1 = bf16[64,768]{1,0:T(8,128)(2,1)S(1)} copy-done((bf16[64,768]{1,0:T(8,128)(2,1)S(1)}, bf16[64,768]{1,0:T(8,128)(2,1)}, u32[]{:S(2)}) %copy-start.1) | copy-done | bytes 98328
  2.9 0.0 copy-start.2
  2.9 0.7 %copy-done.2 = s32[64,1]{0,1:T(1,128)S(1)} copy-done((s32[64,1]{0,1:T(1,128)S(1)}, s32[64,1]{0,1:T(1,128)}, u32[]{:S(2)}) %copy-start.2) | copy-done | bytes 280
  3.6 38.0 %shard_map.50 = (f32[8,128]{1,0:T(8,128)S(1)}, f32[1,128]{1,0:T(1,128)S(1)}) custom-call(bf16[1024,768]{1,0:T(8,128)(2,1)S(1)} %copy-done, bf16[64,768]{1,0:T(8,128)(2,1)S(1)} %copy-done.1, s32[1,64]{1,0:T(1,128)S(1)} %bitcast.4), custom_call_target="tpu_custom_call" | custom-call | tf_op jit(solution)/shard_map/pallas_call | solution.py:234
  41.6 0.6 %copy.7 = f32[1024]{0:T(1024)} copy(f32[1024]{0:T(1024)S(1)} %bitcast.3) | data formatting | bytes 8192
  42.2 0.5 %copy.8 = f32[128]{0:T(128)} copy(f32[128]{0:T(128)S(1)} %bitcast.5) | data formatting | bytes 1024
Async XLA Ops:
  0.6 1.4 %copy-start = (bf16[1024,768]{1,0:T(8,128)(2,1)S(1)}, bf16[1024,768]{1,0:T(8,128)(2,1)}, u32[]{:S(2)}) copy-start(bf16[1024,768]{1,0:T(8,128)(2,1)} %docs_hbm.1) | copy-start | bytes 4718596
  2.0 0.9 %copy-start.1 = (bf16[64,768]{1,0:T(8,128)(2,1)S(1)}, bf16[64,768]{1,0:T(8,128)(2,1)}, u32[]{:S(2)}) copy-start(bf16[64,768]{1,0:T(8,128)(2,1)} %eval_ref.1) | copy-start | bytes 294916
  2.9 0.7 %copy-start.2 = (s32[64,1]{0,1:T(1,128)S(1)}, s32[64,1]{0,1:T(1,128)}, u32[]{:S(2)}) copy-start(s32[64,1]{0,1:T(1,128)} %param.5) | copy-start | bytes 772

commit v5 on v4

--- a/solution.py
+++ b/solution.py
@@ -105,8 +105,13 @@
             arrivals.append(lax.rem(place[dim] - sign * step + n, n))
         waiting.append((q, fixed, dim, later, step, copies, arrivals[:1] if split else arrivals))
 
+    def forwarding():
+        return [event for event in waiting if event[3] or event[4] < sizes[event[2]] // 2]
+
     def advance():
-        q, fixed, dim, later, step, copies, arrivals = waiting.pop(0)
+        event = forwarding()[0]
+        waiting[:] = [other for other in waiting if other is not event]
+        q, fixed, dim, later, step, copies, arrivals = event
         for copy in copies:
             copy.wait_recv()
         emit(q, fixed, dim, later, step + 1)
@@ -124,7 +129,7 @@
                 for k in range(1, C)
             ]
 
-    for _ in range(len(waiting)):
+    for _ in range(len(forwarding())):
         advance()
     for copy in id_copies:
         copy.wait_recv()
@@ -143,9 +148,9 @@
             doc_scale[c, rows, :] = jnp.broadcast_to(to_scale(sums, width), (TILE, LANES))
             row_max[c, rows, :] = jnp.full((TILE, LANES), -jnp.inf, jnp.float32)
 
-        for _ in range(len(waiting) // 2):
+        for _ in range(len(forwarding()) // 2):
             advance()
-    while waiting:
+    while forwarding():
         advance()
     for copy in id_copies:
         copy.wait_recv()
@@ -160,6 +165,10 @@
     owner_lane = lax.broadcasted_iota(jnp.int32, (owners, chunk), 1)
     bench = lax.broadcasted_iota(jnp.int32, (NBENCH, chunk), 0).astype(jnp.float32)
     for q in range(PARTS):
+        for event in waiting:
+            if event[0] == q:
+                for copy in event[5]:
+                    copy.wait_recv()
         questions = held[q].reshape(chunk, width)
         sums = jnp.sum(square_sums(questions).T, axis=0, keepdims=True)
         eval_scale = to_scale(sums, width)

time: 42.9 us -> 41 us (0.956)
  Pallas kernels: 38 us -> 36.1 us
    pallas_call x1, Pallas kernels: 38 us -> 36.1 us  [body(): pl.pallas_call(functools.partial(kernel, dims), out_shape=(jax.ShapeDtype...]
where the time goes in v5:
time: 41 us; the launch traced here: 40.8 us
  Pallas kernels  36.1 us (88%)
  local copies, waits for them, and re-layouts  4.05 us (10%)
  between operations  0.65 us (2%)
    pallas_call x1, Pallas kernels, body(): pl.pallas_call(functools.partial(kernel, dims), out_shape=(jax.ShapeDtype...  36.1 us
    unnamed x8, local copies, waits for them, and re-layouts  4.05 us

profile of v5, /device:TPU:0, one launch (start us, length us, event | category | flops | bytes accessed | tf_op | source)
XLA Modules:
  0.0 40.8 jit_solution(8934425719344116528)
XLA Ops:
  0.6 0.0 copy-start
  0.6 1.4 %copy-done = bf16[1024,768]{1,0:T(8,128)(2,1)S(1)} copy-done((bf16[1024,768]{1,0:T(8,128)(2,1)S(1)}, bf16[1024,768]{1,0:T(8,128)(2,1)}, u32[]{:S(2)}) %copy-start) | copy-done | bytes 1572888
  2.0 0.0 copy-start.1
  2.0 0.9 %copy-done.1 = bf16[64,768]{1,0:T(8,128)(2,1)S(1)} copy-done((bf16[64,768]{1,0:T(8,128)(2,1)S(1)}, bf16[64,768]{1,0:T(8,128)(2,1)}, u32[]{:S(2)}) %copy-start.1) | copy-done | bytes 98328
  2.9 0.0 copy-start.2
  2.9 0.7 %copy-done.2 = s32[64,1]{0,1:T(1,128)S(1)} copy-done((s32[64,1]{0,1:T(1,128)S(1)}, s32[64,1]{0,1:T(1,128)}, u32[]{:S(2)}) %copy-start.2) | copy-done | bytes 280
  3.6 36.1 %shard_map.50 = (f32[8,128]{1,0:T(8,128)S(1)}, f32[1,128]{1,0:T(1,128)S(1)}) custom-call(bf16[1024,768]{1,0:T(8,128)(2,1)S(1)} %copy-done, bf16[64,768]{1,0:T(8,128)(2,1)S(1)} %copy-done.1, s32[1,64]{1,0:T(1,128)S(1)} %bitcast.4), custom_call_target="tpu_custom_call" | custom-call | tf_op jit(solution)/shard_map/pallas_call | solution.py:243
  39.7 0.6 %copy.7 = f32[1024]{0:T(1024)} copy(f32[1024]{0:T(1024)S(1)} %bitcast.3) | data formatting | bytes 8192
  40.3 0.5 %copy.8 = f32[128]{0:T(128)} copy(f32[128]{0:T(128)S(1)} %bitcast.5) | data formatting | bytes 1024
Async XLA Ops:
  0.6 1.4 %copy-start = (bf16[1024,768]{1,0:T(8,128)(2,1)S(1)}, bf16[1024,768]{1,0:T(8,128)(2,1)}, u32[]{:S(2)}) copy-start(bf16[1024,768]{1,0:T(8,128)(2,1)} %docs_hbm.1) | copy-start | bytes 4718596
  2.0 0.9 %copy-start.1 = (bf16[64,768]{1,0:T(8,128)(2,1)S(1)}, bf16[64,768]{1,0:T(8,128)(2,1)}, u32[]{:S(2)}) copy-start(bf16[64,768]{1,0:T(8,128)(2,1)} %eval_ref.1) | copy-start | bytes 294916
  2.9 0.7 %copy-start.2 = (s32[64,1]{0,1:T(1,128)S(1)}, s32[64,1]{0,1:T(1,128)}, u32[]{:S(2)}) copy-start(s32[64,1]{0,1:T(1,128)} %param.5) | copy-start | bytes 772
